TPU v7x, 32 devices: a whole 2x2x4 slice. The times are simulated.
32 devices in a mesh: dp: 8 (over y, x, core), tensor: 4 (over z).
Axes of the slice: x: 2, y: 2, z: 4, core: 2. Of those that a mesh axis runs over, the one named last changes fastest.
Arguments:
- layer_input: bfloat16 [1024, 8, 2048], P('tensor', 'dp'), may hold values from -6 to 6
- first_gain: bfloat16 [2048], replicated, may hold values from 0.25 to 1.75
- query_weight: bfloat16 [2048, 2048], P('dp', 'tensor'), may hold values from -0.125 to 0.125
- key_matrix: bfloat16 [2048, 1024], P('dp', 'tensor'), may hold values from -0.125 to 0.125
- value_matrix: bfloat16 [2048, 1024], P('dp', 'tensor'), may hold values from -0.125 to 0.125
- query_gain: bfloat16 [128], replicated, may hold values from 0.6 to 7
- key_gain: bfloat16 [128], replicated, may hold values from 0.6 to 7
- output_weight: bfloat16 [2048, 2048], P('dp', 'tensor'), may hold values from -0.75 to 0.75
- second_gain: bfloat16 [2048], replicated, may hold values from 0.25 to 1.75
- gate_weight: bfloat16 [2048, 6144], P('dp', 'tensor'), may hold values from -0.125 to 0.125
- up_weight: bfloat16 [2048, 6144], P('dp', 'tensor'), may hold values from -0.125 to 0.125
- down_weight: bfloat16 [2048, 6144], P('dp', 'tensor'), may hold values from -0.078125 to 0.078125
- segments: int32 [8, 1024], P('dp'), may hold values from 0 to 3, never falling along the last dimension, each value on 1 to 512 neighbouring positions
- cotangent: bfloat16 [1024, 8, 2048], P('tensor', 'dp'), may hold values from -6 to 6
Outputs:
- layer_output: bfloat16 [1024, 8, 2048], P('tensor', 'dp')
- input_grad: bfloat16 [1024, 8, 2048], P('tensor', 'dp')
- first_gain_grad: float32 [2048], replicated
- query_weight_grad: float32 [2048, 2048], P('dp', 'tensor')
- key_weight_grad: float32 [2048, 1024], P('dp', 'tensor')
- value_weight_grad: float32 [2048, 1024], P('dp', 'tensor')
- query_gain_grad: float32 [128], replicated
- key_gain_grad: float32 [128], replicated
- output_weight_grad: float32 [2048, 2048], P('dp', 'tensor')
- second_gain_grad: float32 [2048], replicated
- gate_weight_grad: float32 [2048, 6144], P('dp', 'tensor')
- up_weight_grad: float32 [2048, 6144], P('dp', 'tensor')
- down_weight_grad: float32 [2048, 6144], P('dp', 'tensor')
Inputs may be any that keep to these rules, and one draw needn't show every extreme that they name: `segments`: along each sequence the segment numbers never fall; every number appears, each document holds 1 to 512 positions and one holds exactly 512.
All inputs are finite; a program needn't handle non-finite values.
Results may differ from a plain program's by a relative error of at most 0.025.
The roundings to bfloat16 on the way count: a program that leaves them out, or rounds other values in their place, can miss the bound.
Values may be sent and summed in bfloat16 or wider, within the bound.
A program may use at most 192 MiB of HBM per device.

v0:
```python
import jax
import jax.numpy as jnp
from jax import lax
from jax.sharding import PartitionSpec as P

epsilon = 1e-06
rope_base = 1000000.0


def rms_parts(values, gain):
    inverse = lax.rsqrt(jnp.mean(values * values, axis=-1, keepdims=True) + epsilon)
    return (values * inverse * gain, inverse)


def rms_back(values, inverse, gain, upstream):
    normed = values * inverse
    inner_term = upstream * gain
    value_grad = inverse * (
        inner_term - normed * jnp.mean(inner_term * normed, axis=-1, keepdims=True)
    )
    return (value_grad, upstream * normed)


def rope_tables(sequence_length, head_size):
    half_width = head_size // 2
    frequency = rope_base ** (-(2.0 * jnp.arange(half_width, dtype=jnp.float32)) / head_size)
    angles = jnp.arange(sequence_length, dtype=jnp.float32)[:, None] * frequency[None, :]
    angles = jnp.concatenate([angles, angles], axis=1)
    return (jnp.cos(angles), jnp.sin(angles))


def rotate(values, cosine_table, sine_table):
    half_width = values.shape[-1] // 2
    turned = jnp.concatenate([-values[..., half_width:], values[..., :half_width]], axis=-1)
    return values * cosine_table + turned * sine_table


def rotate_back(upstream, cosine_table, sine_table):
    half_width = upstream.shape[-1] // 2
    shifted = upstream * sine_table
    return upstream * cosine_table + jnp.concatenate(
        [shifted[..., half_width:], -shifted[..., :half_width]], axis=-1
    )


def allowed_pairs(segment_row):
    position = jnp.arange(segment_row.shape[0])
    return (segment_row[:, None] == segment_row[None, :]) & (position[None, :] <= position[:, None])


def masked_scores(query_row_block, key_rows, allowed):
    factor = query_row_block.shape[-1] ** (-0.5)
    scores = (
        jnp.einsum("qhgd,khd->hgqk", query_row_block, key_rows, preferred_element_type=jnp.float32)
        * factor
    )
    return jnp.where(allowed, scores, -1e30)


def attend_forward(query_row_block, key_rows, value_rows, allowed):
    scores = masked_scores(query_row_block, key_rows, allowed)
    row_max = jnp.max(scores, axis=-1, keepdims=True)
    weights = jnp.exp(scores - row_max)
    row_total = jnp.sum(weights, axis=-1, keepdims=True)
    attention = (weights / row_total).astype(jnp.bfloat16)
    out_rows = jnp.einsum(
        "hgqk,khd->qhgd", attention, value_rows, preferred_element_type=jnp.float32
    )
    return (out_rows, row_max + jnp.log(row_total))


def attend_backward(query_row_block, key_rows, value_rows, allowed, log_total, grad_out):
    scores = masked_scores(query_row_block, key_rows, allowed)
    attention = jnp.exp(scores - log_total)
    grad_attention = jnp.einsum(
        "qhgd,khd->hgqk", grad_out, value_rows, preferred_element_type=jnp.float32
    )
    row_delta = jnp.sum(attention * grad_attention, axis=-1, keepdims=True)
    grad_scores = (attention * (grad_attention - row_delta)).astype(jnp.bfloat16)
    factor = query_row_block.shape[-1] ** (-0.5)
    grad_query = (
        jnp.einsum("hgqk,khd->qhgd", grad_scores, key_rows, preferred_element_type=jnp.float32)
        * factor
    )
    grad_key = (
        jnp.einsum(
            "hgqk,qhgd->khd", grad_scores, query_row_block, preferred_element_type=jnp.float32
        )
        * factor
    )
    grad_value = jnp.einsum(
        "hgqk,qhgd->khd",
        attention.astype(jnp.bfloat16),
        grad_out,
        preferred_element_type=jnp.float32,
    )
    return (
        grad_query.astype(jnp.bfloat16),
        grad_key.astype(jnp.bfloat16),
        grad_value.astype(jnp.bfloat16),
    )


def fetch_attention(query_weight, key_matrix, value_matrix, output_weight):
    return (
        lax.all_gather(query_weight, "dp", axis=0, tiled=True),
        lax.all_gather(key_matrix, "dp", axis=0, tiled=True),
        lax.all_gather(value_matrix, "dp", axis=0, tiled=True),
        lax.all_gather(output_weight, "dp", axis=0, tiled=True),
    )


def fetch_feedforward(gate_weight, up_weight, down_weight):
    return (
        lax.all_gather(gate_weight, "dp", axis=0, tiled=True),
        lax.all_gather(up_weight, "dp", axis=0, tiled=True),
        lax.all_gather(down_weight, "dp", axis=0, tiled=True),
    )


def gather_rows(values):
    return lax.all_gather(values, "tensor", axis=0, tiled=True)


def gather_cotangent(values):
    return lax.all_gather(values, "tensor", axis=0, tiled=True)


def branch_total(term_fn, short_rows):
    return lax.psum_scatter(
        term_fn(jnp.int32(0), short_rows * lax.axis_size("tensor")).astype(jnp.bfloat16),
        "tensor",
        scatter_dimension=0,
        tiled=True,
    ).astype(jnp.float32)


def input_total(term_fn, short_rows):
    return lax.psum_scatter(
        term_fn(jnp.int32(0), short_rows * lax.axis_size("tensor")).astype(jnp.bfloat16),
        "tensor",
        scatter_dimension=0,
        tiled=True,
    ).astype(jnp.float32)


def project_rows(left, right):
    return jnp.einsum("lsc,dc->lsd", left, right, preferred_element_type=jnp.float32)


def weight_term(rows_in, grads_in):
    return jnp.einsum("lsd,lsc->dc", rows_in, grads_in, preferred_element_type=jnp.float32)


def body(
    layer_input,
    first_gain,
    query_weight,
    key_matrix,
    value_matrix,
    query_gain,
    key_gain,
    output_weight,
    second_gain,
    gate_weight,
    up_weight,
    down_weight,
    segments,
    cotangent,
):
    short_rows = layer_input.shape[0]
    sequence_length = short_rows * lax.axis_size("tensor")
    seq_count = layer_input.shape[1]
    head_size = query_gain.shape[0]
    kv_heads = key_matrix.shape[1] // head_size
    query_heads = query_weight.shape[1] // head_size
    head_groups = query_heads // kv_heads
    cosine_table, sine_table = rope_tables(sequence_length, head_size)
    cos_heads = cosine_table[:, None, None, :]
    sin_heads = sine_table[:, None, None, :]
    gain_one = first_gain.astype(jnp.float32)
    gain_two = second_gain.astype(jnp.float32)
    gain_query = query_gain.astype(jnp.float32)
    gain_key = key_gain.astype(jnp.float32)
    query_full, key_full, value_full, output_full = fetch_attention(
        query_weight, key_matrix, value_matrix, output_weight
    )
    source = layer_input.astype(jnp.float32)
    first_normalized, inverse_one = rms_parts(source, gain_one)
    rows_one = gather_rows(first_normalized.astype(jnp.bfloat16))
    proj_query = jnp.einsum("lsd,dc->lsc", rows_one, query_full, preferred_element_type=jnp.float32)
    proj_query = proj_query.reshape(sequence_length, seq_count, query_heads, head_size)
    projected_key = jnp.einsum(
        "lsd,dc->lsc", rows_one, key_full, preferred_element_type=jnp.float32
    )
    projected_key = projected_key.reshape(sequence_length, seq_count, kv_heads, head_size)
    projected_value = jnp.einsum(
        "lsd,dc->lsc", rows_one, value_full, preferred_element_type=jnp.float32
    )
    projected_value = projected_value.reshape(sequence_length, seq_count, kv_heads, head_size)
    unit_query, inverse_query = rms_parts(proj_query, gain_query)
    unit_key, inverse_key = rms_parts(projected_key, gain_key)
    query_row_block = rotate(unit_query, cos_heads, sin_heads).astype(jnp.bfloat16)
    key_rows = rotate(unit_key, cos_heads, sin_heads).astype(jnp.bfloat16)
    value_rows = projected_value.astype(jnp.bfloat16)
    member = 0
    allowed = allowed_pairs(segments[member])
    out_rows, log_total = attend_forward(
        query_row_block[:, member].reshape(sequence_length, kv_heads, head_groups, head_size),
        key_rows[:, member],
        value_rows[:, member],
        allowed,
    )
    attended_list = [out_rows.reshape(sequence_length, query_heads * head_size)]
    log_totals = [log_total]
    masks = [allowed]
    attended = jnp.stack(attended_list, axis=1).astype(jnp.bfloat16)
    branch = branch_total(
        lambda row_start, row_count: project_rows(attended, output_full), short_rows
    )
    middle = source + branch
    gate_complete, up_complete, down_complete = fetch_feedforward(
        gate_weight, up_weight, down_weight
    )
    normed_two, inverse_two = rms_parts(middle, gain_two)
    second_rows = gather_rows(normed_two.astype(jnp.bfloat16))
    gate_projected = jnp.einsum(
        "qpt,to->qpo", second_rows, gate_complete, preferred_element_type=jnp.float32
    )
    up_projected = jnp.einsum(
        "qpt,to->qpo", second_rows, up_complete, preferred_element_type=jnp.float32
    )
    sigmoid_gate = jax.nn.sigmoid(gate_projected)
    activated = gate_projected * sigmoid_gate
    hidden = (activated * up_projected).astype(jnp.bfloat16)
    mixed = branch_total(
        lambda row_start, row_count: project_rows(hidden, down_complete), short_rows
    )
    layer_output = (middle + mixed).astype(jnp.bfloat16)
    gate_complete, up_complete, down_complete = fetch_feedforward(
        gate_weight, up_weight, down_weight
    )
    gradient_rows = gather_cotangent(cotangent)
    grad_hidden = jnp.einsum(
        "qpt,to->qpo", gradient_rows, down_complete, preferred_element_type=jnp.float32
    )
    down_grad = weight_term(gradient_rows, hidden)
    grad_gate = (
        grad_hidden * up_projected * sigmoid_gate * (1.0 + gate_projected * (1.0 - sigmoid_gate))
    ).astype(jnp.bfloat16)
    grad_up = (grad_hidden * activated).astype(jnp.bfloat16)
    gate_grad = weight_term(second_rows, grad_gate)
    up_grad = weight_term(second_rows, grad_up)
    grad_two = input_total(
        lambda row_start, row_count: project_rows(grad_gate, gate_complete)
        + project_rows(grad_up, up_complete),
        short_rows,
    )
    grad_mid_norm, gain_two_terms = rms_back(middle, inverse_two, gain_two, grad_two)
    grad_middle = cotangent.astype(jnp.float32) + grad_mid_norm
    query_full, key_full, value_full, output_full = fetch_attention(
        query_weight, key_matrix, value_matrix, output_weight
    )
    branch_rows = gather_cotangent(grad_middle.astype(jnp.bfloat16))
    grad_attended = jnp.einsum(
        "lsd,dc->lsc", branch_rows, output_full, preferred_element_type=jnp.float32
    ).astype(jnp.bfloat16)
    output_grad = weight_term(branch_rows, attended)
    member = 0
    grad_query, grad_key, grad_value = attend_backward(
        query_row_block[:, member].reshape(sequence_length, kv_heads, head_groups, head_size),
        key_rows[:, member],
        value_rows[:, member],
        masks[member],
        log_totals[member],
        grad_attended[:, member].reshape(sequence_length, kv_heads, head_groups, head_size),
    )
    query_list = [grad_query.reshape(sequence_length, query_heads, head_size)]
    key_list = [grad_key]
    value_list = [grad_value]
    grad_query_rows = jnp.stack(query_list, axis=1).astype(jnp.float32)
    grad_key_rows = jnp.stack(key_list, axis=1).astype(jnp.float32)
    grad_value_low = jnp.stack(value_list, axis=1).reshape(
        sequence_length, seq_count, kv_heads * head_size
    )
    grad_proj_query, query_gain_terms = rms_back(
        proj_query, inverse_query, gain_query, rotate_back(grad_query_rows, cos_heads, sin_heads)
    )
    grad_proj_key, key_gain_terms = rms_back(
        projected_key, inverse_key, gain_key, rotate_back(grad_key_rows, cos_heads, sin_heads)
    )
    grad_query_low = grad_proj_query.reshape(
        sequence_length, seq_count, query_heads * head_size
    ).astype(jnp.bfloat16)
    grad_key_low = grad_proj_key.reshape(sequence_length, seq_count, kv_heads * head_size).astype(
        jnp.bfloat16
    )
    query_grad = weight_term(rows_one, grad_query_low)
    key_grad = weight_term(rows_one, grad_key_low)
    value_grad = weight_term(rows_one, grad_value_low)
    grad_one = input_total(
        lambda row_start, row_count: project_rows(grad_query_low, query_full)
        + project_rows(grad_key_low, key_full)
        + project_rows(grad_value_low, value_full),
        short_rows,
    )
    grad_src_norm, gain_one_terms = rms_back(source, inverse_one, gain_one, grad_one)
    input_grad = (grad_middle + grad_src_norm).astype(jnp.bfloat16)
    gain_sums = lax.psum(
        (
            jnp.sum(gain_one_terms, axis=(0, 1)),
            jnp.sum(gain_two_terms, axis=(0, 1)),
            jnp.sum(query_gain_terms, axis=(0, 1, 2)),
            jnp.sum(key_gain_terms, axis=(0, 1, 2)),
        ),
        ("dp", "tensor"),
    )
    weight_sums = (
        lax.psum_scatter(
            query_grad.astype(jnp.bfloat16), "dp", scatter_dimension=0, tiled=True
        ).astype(jnp.float32),
        lax.psum_scatter(
            key_grad.astype(jnp.bfloat16), "dp", scatter_dimension=0, tiled=True
        ).astype(jnp.float32),
        lax.psum_scatter(
            value_grad.astype(jnp.bfloat16), "dp", scatter_dimension=0, tiled=True
        ).astype(jnp.float32),
        lax.psum_scatter(
            output_grad.astype(jnp.bfloat16), "dp", scatter_dimension=0, tiled=True
        ).astype(jnp.float32),
        lax.psum_scatter(
            gate_grad.astype(jnp.bfloat16), "dp", scatter_dimension=0, tiled=True
        ).astype(jnp.float32),
        lax.psum_scatter(
            up_grad.astype(jnp.bfloat16), "dp", scatter_dimension=0, tiled=True
        ).astype(jnp.float32),
        lax.psum_scatter(
            down_grad.astype(jnp.bfloat16), "dp", scatter_dimension=0, tiled=True
        ).astype(jnp.float32),
    )
    return (
        layer_output,
        input_grad,
        gain_sums[0],
        weight_sums[0],
        weight_sums[1],
        weight_sums[2],
        gain_sums[2],
        gain_sums[3],
        weight_sums[3],
        gain_sums[1],
        weight_sums[4],
        weight_sums[5],
        weight_sums[6],
    )


def solution(mesh):
    return jax.shard_map(
        body,
        mesh=mesh,
        in_specs=(
            P("tensor", "dp", None),
            P(),
            P("dp", "tensor"),
            P("dp", "tensor"),
            P("dp", "tensor"),
            P(),
            P(),
            P("dp", "tensor"),
            P(),
            P("dp", "tensor"),
            P("dp", "tensor"),
            P("dp", "tensor"),
            P("dp", None),
            P("tensor", "dp", None),
        ),
        out_specs=(
            P("tensor", "dp", None),
            P("tensor", "dp", None),
            P(),
            P("dp", "tensor"),
            P("dp", "tensor"),
            P("dp", "tensor"),
            P(),
            P(),
            P("dp", "tensor"),
            P(),
            P("dp", "tensor"),
            P("dp", "tensor"),
            P("dp", "tensor"),
        ),
        check_vma=False,
    )
```

profile of v0, /device:TPU:0, one launch (start us, length us, event | category | flops | bytes accessed | tf_op | source)
XLA Modules:
  0.0 1326.5 jit_solution(12982953722708710317)
XLA Ops:
  15.4 2.7 fusion.104
  19.7 16.4 %all-gather.14.cloned.1.call-done = bf16[2048,256]{1,0:T(8,128)(2,1)} async-done(((bf16[256,256]{1,0:T(8,128)(2,1)}), bf16[2048,256]{1,0:T(8,128)(2,1)}) %all-gather.14.cloned.1.call-update) | async-done | bytes 1048592 | tf_op jit(solution)/shard_map/all_gather | solution.py:108
  38.3 23.0 %all-gather.16.cloned.1.call-done = bf16[2048,256]{1,0:T(8,128)(2,1)} async-done(((bf16[256,256]{1,0:T(8,128)(2,1)}), bf16[2048,256]{1,0:T(8,128)(2,1)}) %all-gather.16.cloned.1.call-update) | async-done | bytes 1048592 | tf_op jit(solution)/shard_map/all_gather | solution.py:107
  61.3 82.9 %all-gather.12.cloned.1.call-done = bf16[1024,1,2048]{2,0,1:T(8,128)(2,1)} async-done(((bf16[256,1,2048]{2,0,1:T(8,128)(2,1)}), bf16[1024,1,2048]{2,0,1:T(8,128)(2,1)}) %all-gather.12.cloned.1.call-update) | async-done | bytes 4194320 | tf_op jit(solution)/shard_map/all_gather | solution.py:122
  144.2 3.8 fusion.33
  149.5 22.8 %all-gather.18.cloned.1.call-done = bf16[2048,512]{1,0:T(8,128)(2,1)} async-done(((bf16[256,512]{1,0:T(8,128)(2,1)}), bf16[2048,512]{1,0:T(8,128)(2,1)}) %all-gather.18.cloned.1.call-update) | async-done | bytes 2097168 | tf_op jit(solution)/shard_map/all_gather | solution.py:106
  172.3 5.2 fusion.31
  184.9 7.9 fusion.107
  192.7 8.0 fusion.3
  200.8 7.6 fusion.77
  209.4 6.0 convert_bitcast_fusion.1
  216.2 76.4 %reduce-scatter.12.cloned.1.call-done = bf16[256,1,2048]{2,0,1:T(8,128)(2,1)} async-done(((bf16[1024,1,2048]{2,0,1:T(8,128)(2,1)}), bf16[256,1,2048]{2,0,1:T(8,128)(2,1)}) %reduce-scatter.12.cloned.1.call-update) | async-done | bytes 1048592 | tf_op jit(solution)/shard_map/reduce_scatter | solution.py:130
  298.9 41.5 %all-gather.26.cloned.1.call-done = bf16[2048,1536]{1,0:T(8,128)(2,1)} async-done(((bf16[256,1536]{1,0:T(8,128)(2,1)}), bf16[2048,1536]{1,0:T(8,128)(2,1)}) %all-gather.26.cloned.1.call-update) | async-done | bytes 6291472 | tf_op jit(solution)/shard_map/all_gather | solution.py:116
  340.4 82.9 %all-gather.22.cloned.1.call-done = bf16[1024,1,2048]{2,0,1:T(8,128)(2,1)} async-done(((bf16[256,1,2048]{2,0,1:T(8,128)(2,1)}), bf16[1024,1,2048]{2,0,1:T(8,128)(2,1)}) %all-gather.22.cloned.1.call-update) | async-done | bytes 4194320 | tf_op jit(solution)/shard_map/all_gather | solution.py:122
  423.3 11.9 fusion.21
  435.2 33.9 %all-gather.24.cloned.1.call-done = bf16[2048,1536]{1,0:T(8,128)(2,1)} async-done(((bf16[256,1536]{1,0:T(8,128)(2,1)}), bf16[2048,1536]{1,0:T(8,128)(2,1)}) %all-gather.24.cloned.1.call-update) | async-done | bytes 6291472 | tf_op jit(solution)/shard_map/all_gather | solution.py:115
  469.1 11.8 fusion.23
  480.9 70.4 %all-gather.30.cloned.1.call-done = bf16[1024,1,2048]{2,0,1:T(8,128)(2,1)} async-done(((bf16[256,1,2048]{2,0,1:T(8,128)(2,1)}), bf16[1024,1,2048]{2,0,1:T(8,128)(2,1)}) %all-gather.30.cloned.1.call-update) | async-done | bytes 4194320 | tf_op jit(solution)/shard_map/all_gather | solution.py:126
  551.3 45.8 %all-gather.28.cloned.1.call-done = bf16[2048,1536]{1,0:T(8,128)(2,1)} async-done(((bf16[256,1536]{1,0:T(8,128)(2,1)}), bf16[2048,1536]{1,0:T(8,128)(2,1)}) %all-gather.28.cloned.1.call-update) | async-done | bytes 6291472 | tf_op jit(solution)/shard_map/all_gather | solution.py:117
  597.1 16.8 %multiply_convert_fusion = (bf16[1024,1536]{1,0:T(8,128)(2,1)}, bf16[1024,1536]{1,0:T(8,128)(2,1)S(1)}, bf16[1024,1536]{1,0:T(8,128)(2,1)}) fusion(f32[1024,1536]{1,0:T(8,128)} %fusion.23, f32[1024,1536]{1,0:T(8,128)} %fusion.21, bf16[2048,1536]{1,0:T(8,128)(2,1)} %all-gather.28.cloned.1.call-done, bf16[1024,1,2048]{2,0,1:T(8,128)(2,1)} %all-gather.30.cloned.1.call-done), kind=kOutput, calls=%fused_computation.20 | convolution fusion | flops 6466043904 | bytes 32505856 | tf_op jit(solution)/shard_map/qpt,to->qpo/dot_general | solution.py:244
  613.9 6.7 fusion.108
  620.6 11.1 fusion.11
  631.8 76.9 %reduce-scatter.16.cloned.1.call-done = bf16[256,1,2048]{2,0,1:T(8,128)(2,1)} async-done(((bf16[1024,1,2048]{2,0,1:T(8,128)(2,1)}), bf16[256,1,2048]{2,0,1:T(8,128)(2,1)}) %reduce-scatter.16.cloned.1.call-update) | async-done | bytes 1048592 | tf_op jit(solution)/shard_map/reduce_scatter | solution.py:139
  713.1 11.4 fusion.9
  724.6 12.2 convolution_convert_fusion.1
  736.8 11.4 convolution_convert_fusion.2
  748.5 45.9 %all-gather.32.cloned.1.call-done = bf16[1024,1,2048]{2,0,1:T(8,128)(2,1)} async-done(((bf16[256,1,2048]{2,0,1:T(8,128)(2,1)}), bf16[1024,1,2048]{2,0,1:T(8,128)(2,1)}) %all-gather.32.cloned.1.call-update) | async-done | bytes 4194320 | tf_op jit(solution)/shard_map/all_gather | solution.py:126
  794.4 5.2 fusion.79
  799.7 11.1 fusion.89
  814.1 7.9 fusion
  822.0 8.3 fusion.2
  830.3 3.3 copy-done.2
  833.6 5.2 fusion.88
  845.8 6.4 fusion.46
  852.3 4.8 fusion.78
  866.1 3.7 fusion.43
  874.9 3.4 fusion.38
  878.4 11.2 convert_bitcast_fusion
  892.2 30.6 %reduce-scatter.30.cloned.1.call-done = bf16[256,1536]{1,0:T(8,128)(2,1)} async-done(((bf16[2048,1536]{1,0:T(8,128)(2,1)}), bf16[256,1536]{1,0:T(8,128)(2,1)}) %reduce-scatter.30.cloned.1.call-update) | async-done | bytes 786448 | tf_op jit(solution)/shard_map/reduce_scatter | solution.py:334
  925.3 62.6 %reduce-scatter.28.cloned.1.call-done = bf16[256,1536]{1,0:T(8,128)(2,1)} async-done(((bf16[2048,1536]{1,0:T(8,128)(2,1)}), bf16[256,1536]{1,0:T(8,128)(2,1)}) %reduce-scatter.28.cloned.1.call-update) | async-done | bytes 786448 | tf_op jit(solution)/shard_map/reduce_scatter | solution.py:331
  990.3 36.6 %reduce-scatter.24.cloned.1.call-done = bf16[256,256]{1,0:T(8,128)(2,1)} async-done(((bf16[2048,256]{1,0:T(8,128)(2,1)}), bf16[256,256]{1,0:T(8,128)(2,1)}) %reduce-scatter.24.cloned.1.call-update) | async-done | bytes 131088 | tf_op jit(solution)/shard_map/reduce_scatter | solution.py:325
  1028.5 37.4 %reduce-scatter.22.cloned.1.call-done = bf16[256,256]{1,0:T(8,128)(2,1)} async-done(((bf16[2048,256]{1,0:T(8,128)(2,1)}), bf16[256,256]{1,0:T(8,128)(2,1)}) %reduce-scatter.22.cloned.1.call-update) | async-done | bytes 131088 | tf_op jit(solution)/shard_map/reduce_scatter | solution.py:322
  1067.5 42.8 %reduce-scatter.26.cloned.1.call-done = bf16[256,512]{1,0:T(8,128)(2,1)} async-done(((bf16[2048,512]{1,0:T(8,128)(2,1)}), bf16[256,512]{1,0:T(8,128)(2,1)}) %reduce-scatter.26.cloned.1.call-update) | async-done | bytes 262160 | tf_op jit(solution)/shard_map/reduce_scatter | solution.py:328
  1112.1 42.5 %reduce-scatter.20.cloned.1.call-done = bf16[256,512]{1,0:T(8,128)(2,1)} async-done(((bf16[2048,512]{1,0:T(8,128)(2,1)}), bf16[256,512]{1,0:T(8,128)(2,1)}) %reduce-scatter.20.cloned.1.call-update) | async-done | bytes 262160 | tf_op jit(solution)/shard_map/reduce_scatter | solution.py:319
  1156.4 77.3 %reduce-scatter.18.cloned.1.call-done = bf16[256,1,2048]{2,0,1:T(8,128)(2,1)} async-done(((bf16[1024,1,2048]{2,0,1:T(8,128)(2,1)}), bf16[256,1,2048]{2,0,1:T(8,128)(2,1)}) %reduce-scatter.18.cloned.1.call-update) | async-done | bytes 1048592 | tf_op jit(solution)/shard_map/reduce_scatter | solution.py:139
  1235.8 46.5 %all-reduce = (f32[2048]{0:T(1024)}, f32[128]{0:T(128)}, f32[128]{0:T(128)}, f32[2048]{0:T(1024)}) all-reduce(f32[2048]{0:T(1024)S(1)} %get-tuple-element.30, f32[128]{0:T(128)S(1)} %get-tuple-element.26, f32[128]{0:T(128)S(1)} %get-tuple-element.32, f32[2048]{0:T(1024)S(1)} %get-tuple-element.28), channel_id=1, replica_groups=mesh['dp'=8,'tensor'=4] {'dp','tensor'}, use_global_device_ids=true, to_apply=%region_16.17 | all-reduce | flops 4352 | bytes 34816 | tf_op jit(solution)/shard_map/psum | solution.py:309
  1282.3 32.1 %reduce-scatter.14.cloned.1.call-done = bf16[256,1,2048]{2,0,1:T(8,128)(2,1)} async-done(((bf16[1024,1,2048]{2,0,1:T(8,128)(2,1)}), bf16[256,1,2048]{2,0,1:T(8,128)(2,1)}) %reduce-scatter.14.cloned.1.call-update) | async-done | bytes 1048592 | tf_op jit(solution)/shard_map/reduce_scatter | solution.py:130
  1314.4 4.9 fusion.60
  (235 shorter events, 73.9 us)
Async XLA Ops:
  7.2 8.1 copy-start.62
  7.2 8.1 copy-start.63
  7.2 28.8 %all-gather.14.cloned.1.call-start = ((), (), s32[]{:S(2)}) async-start(), calls=%async_computation.12 | async-start | bytes 1179648 | tf_op jit(solution)/shard_map/all_gather | solution.py:108
  7.9 53.4 %all-gather.16.cloned.1.call-start = ((), (), s32[]{:S(2)}) async-start(), calls=%async_computation.13 | async-start | bytes 1179648 | tf_op jit(solution)/shard_map/all_gather | solution.py:107
  8.7 135.5 %all-gather.12.cloned.1.call-start = ((), (), s32[]{:S(2)}) async-start(), calls=%async_computation.11 | async-start | bytes 5242880 | tf_op jit(solution)/shard_map/all_gather | solution.py:122
  9.4 8.7 copy-start.48
  14.0 158.2 %all-gather.18.cloned.1.call-start = ((), (), s32[]{:S(2)}) async-start(), calls=%async_computation.14 | async-start | bytes 2359296 | tf_op jit(solution)/shard_map/all_gather | solution.py:106
  14.6 193.8 %all-gather.20.cloned.1.call-start = ((), (), s32[]{:S(2)}) async-start(), calls=%async_computation.15 | async-start | bytes 2359296 | tf_op jit(solution)/shard_map/all_gather | solution.py:109
  15.2 277.4 %reduce-scatter.12.cloned.1.call-start = ((), (), s32[]{:S(2)}) async-start(), calls=%async_computation.16 | async-start | bytes 5242880 | tf_op jit(solution)/shard_map/reduce_scatter | solution.py:130
  15.3 165.0 %copy-start.51 = (f32[128]{0:T(128)}, f32[128]{0:T(128)S(1)}, u32[]{:S(2)}) copy-start(f32[128]{0:T(128)S(1)} %convert_element_type.245) | copy-start | bytes 1540
  15.3 163.4 %copy-start.53 = (f32[128]{0:T(128)}, f32[128]{0:T(128)S(1)}, u32[]{:S(2)}) copy-start(f32[128]{0:T(128)S(1)} %convert_element_type.243) | copy-start | bytes 1540
  148.0 30.7 %copy-start.4 = (f32[1024,256]{0,1:T(8,128)}, f32[1024,256]{0,1:T(8,128)S(1)}, u32[]{:S(2)}) copy-start(f32[1024,256]{0,1:T(8,128)S(1)} %fusion.33) | copy-start | bytes 3145732
  148.1 30.5 %copy-start.42 = (f32[1024,2]{0,1:T(2,128)}, f32[1024,2]{0,1:T(2,128)S(1)}, u32[]{:S(2)}) copy-start(f32[1024,2]{0,1:T(2,128)S(1)} %add_rsqrt_fusion.1) | copy-start | bytes 24580
  180.2 4.6 copy-start.29
  184.8 15.9 %copy-start.38 = (bf16[1024,2,128,1]{2,0,3,1:T(8,128)(2,1)}, bf16[1024,2,128,1]{2,0,3,1:T(8,128)(2,1)S(1)}, u32[]{:S(2)}) copy-start(bf16[1024,2,128,1]{2,0,3,1:T(8,128)(2,1)S(1)} %fusion.95) | copy-start | bytes 1572868
  215.4 77.2 %copy-start.3 = (bf16[256,1,2048]{2,0,1:T(8,128)(2,1)S(1)}, bf16[256,1,2048]{2,0,1:T(8,128)(2,1)}, u32[]{:S(2)}) copy-start(bf16[256,1,2048]{2,0,1:T(8,128)(2,1)} %param.14) | copy-start | bytes 3145732
  215.4 125.0 %all-gather.26.cloned.1.call-start = ((), (), s32[]{:S(2)}) async-start(), calls=%async_computation.19 | async-start | bytes 7077888 | tf_op jit(solution)/shard_map/all_gather | solution.py:116
  216.1 207.2 %all-gather.22.cloned.1.call-start = ((), (), s32[]{:S(2)}) async-start(), calls=%async_computation.17 | async-start | bytes 5242880 | tf_op jit(solution)/shard_map/all_gather | solution.py:122
  296.8 172.3 %all-gather.24.cloned.1.call-start = ((), (), s32[]{:S(2)}) async-start(), calls=%async_computation.18 | async-start | bytes 7077888 | tf_op jit(solution)/shard_map/all_gather | solution.py:115
  297.6 253.7 %all-gather.30.cloned.1.call-start = ((), (), s32[]{:S(2)}) async-start(), calls=%async_computation.22 | async-start | bytes 5242880 | tf_op jit(solution)/shard_map/all_gather | solution.py:126
  298.2 298.9 %all-gather.28.cloned.1.call-start = ((), (), s32[]{:S(2)}) async-start(), calls=%async_computation.20 | async-start | bytes 7077888 | tf_op jit(solution)/shard_map/all_gather | solution.py:117
  298.9 409.8 %reduce-scatter.16.cloned.1.call-start = ((), (), s32[]{:S(2)}) async-start(), calls=%async_computation.23 | async-start | bytes 5242880 | tf_op jit(solution)/shard_map/reduce_scatter | solution.py:139
  597.1 16.8 %copy-start.56 = (bf16[2048,1536]{1,0:T(8,128)(2,1)S(1)}, bf16[2048,1536]{1,0:T(8,128)(2,1)}, u32[]{:S(2)}) copy-start(bf16[2048,1536]{1,0:T(8,128)(2,1)} %all-gather.24.cloned.1.call-done) | copy-start | bytes 18874372
  613.9 6.7 copy-start.65
  613.9 6.7 copy-start.66
  631.8 77.0 %copy-start.8 = (bf16[256,1,2048]{2,0,1:T(8,128)(2,1)S(1)}, bf16[256,1,2048]{2,0,1:T(8,128)(2,1)}, u32[]{:S(2)}) copy-start(bf16[256,1,2048]{2,0,1:T(8,128)(2,1)} %reduce-scatter.12.cloned.1.call-done) | copy-start | bytes 3145732
  631.8 79.2 %copy-start.19 = (bf16[256,1,2048]{2,0,1:T(8,128)(2,1)S(1)}, bf16[256,1,2048]{2,0,1:T(8,128)(2,1)}, u32[]{:S(2)}) copy-start(bf16[256,1,2048]{2,0,1:T(8,128)(2,1)} %param.27) | copy-start | bytes 3145732
  631.8 162.7 %all-gather.32.cloned.1.call-start = ((), (), s32[]{:S(2)}) async-start(), calls=%async_computation.24 | async-start | bytes 5242880 | tf_op jit(solution)/shard_map/all_gather | solution.py:126
  713.1 176.5 %reduce-scatter.32.cloned.1.call-start = ((), (), s32[]{:S(2)}) async-start(), calls=%async_computation.32 | async-start | bytes 7077888 | tf_op jit(solution)/shard_map/reduce_scatter | solution.py:337
  724.5 198.3 %reduce-scatter.30.cloned.1.call-start = ((), (), s32[]{:S(2)}) async-start(), calls=%async_computation.31 | async-start | bytes 7077888 | tf_op jit(solution)/shard_map/reduce_scatter | solution.py:334
  736.7 251.1 %reduce-scatter.28.cloned.1.call-start = ((), (), s32[]{:S(2)}) async-start(), calls=%async_computation.30 | async-start | bytes 7077888 | tf_op jit(solution)/shard_map/reduce_scatter | solution.py:331
  748.3 278.6 %reduce-scatter.24.cloned.1.call-start = ((), (), s32[]{:S(2)}) async-start(), calls=%async_computation.28 | async-start | bytes 1179648 | tf_op jit(solution)/shard_map/reduce_scatter | solution.py:325
  799.7 11.2 copy-start.24
  799.7 12.0 copy-start.58
  833.6 5.5 copy-start.15
  838.8 227.1 %reduce-scatter.22.cloned.1.call-start = ((), (), s32[]{:S(2)}) async-start(), calls=%async_computation.27 | async-start | bytes 1179648 | tf_op jit(solution)/shard_map/reduce_scatter | solution.py:322
  845.7 6.5 copy-start.52
  845.7 6.5 copy-start.30
  845.8 264.6 %reduce-scatter.26.cloned.1.call-start = ((), (), s32[]{:S(2)}) async-start(), calls=%async_computation.29 | async-start | bytes 2359296 | tf_op jit(solution)/shard_map/reduce_scatter | solution.py:328
  852.2 302.4 %reduce-scatter.20.cloned.1.call-start = ((), (), s32[]{:S(2)}) async-start(), calls=%async_computation.26 | async-start | bytes 2359296 | tf_op jit(solution)/shard_map/reduce_scatter | solution.py:319
  866.1 4.1 copy-start.26
  866.1 4.1 copy-start.33
  869.8 363.9 %reduce-scatter.18.cloned.1.call-start = ((), (), s32[]{:S(2)}) async-start(), calls=%async_computation.25 | async-start | bytes 5242880 | tf_op jit(solution)/shard_map/reduce_scatter | solution.py:139
  878.3 436.1 %reduce-scatter.14.cloned.1.call-start = ((), (), s32[]{:S(2)}) async-start(), calls=%async_computation.21 | async-start | bytes 5242880 | tf_op jit(solution)/shard_map/reduce_scatter | solution.py:130
  892.2 341.6 %copy-start.47 = (f32[2048]{0:T(1024)S(1)}, f32[2048]{0:T(1024)}, u32[]{:S(2)}) copy-start(f32[2048]{0:T(1024)} %copy-done.46) | copy-start | bytes 24580
  892.2 341.6 %copy-start.50 = (f32[256]{0:T(256)S(1)}, f32[256]{0:T(256)}, u32[]{:S(2)}) copy-start(f32[256]{0:T(256)} %copy-done.49) | copy-start | bytes 3076
  925.3 389.1 %copy-start.9 = (bf16[256,1,2048]{2,0,1:T(8,128)(2,1)S(1)}, bf16[256,1,2048]{2,0,1:T(8,128)(2,1)}, u32[]{:S(2)}) copy-start(bf16[256,1,2048]{2,0,1:T(8,128)(2,1)} %reduce-scatter.12.cloned.1.call-done) | copy-start | bytes 3145732
  925.3 389.1 %copy-start.20 = (bf16[256,1,2048]{2,0,1:T(8,128)(2,1)S(1)}, bf16[256,1,2048]{2,0,1:T(8,128)(2,1)}, u32[]{:S(2)}) copy-start(bf16[256,1,2048]{2,0,1:T(8,128)(2,1)} %param.27) | copy-start | bytes 3145732
  (41 other events, 85.5 us)
Sparse Core Ops, SparseCore 0:
  9.9 26.0 all-gather.13
  37.9 23.3 all-gather.15
  63.5 80.7 all-gather.11
  146.0 26.2 all-gather.17
  174.0 27.7 all-gather.19
  215.5 77.0 reduce-scatter.11
  294.4 45.9 all-gather.25
  342.5 80.7 all-gather.21
  425.2 43.8 all-gather.23
  470.5 80.7 all-gather.29
  553.2 43.8 all-gather.27
  631.9 76.7 reduce-scatter.15
  713.2 81.2 all-gather.31
  797.7 60.0 reduce-scatter.31
  861.0 61.7 reduce-scatter.29
  926.0 61.7 reduce-scatter.27
  990.9 35.9 reduce-scatter.23
  1029.9 35.9 reduce-scatter.21
  1069.2 41.1 reduce-scatter.25
  1113.5 41.1 reduce-scatter.19
  1156.9 76.7 reduce-scatter.17
  1236.0 78.3 reduce-scatter.13
where the time goes:
time: 1340 us; the launch traced here: 1330 us
  waiting for transfers between devices  986 us (74%)
  matrix products  192 us (14%)
  other arithmetic  62.4 us (5%)
  blocking collectives  46.5 us (3%)
  local copies, waits for them, and re-layouts  22.1 us (2%)
  between operations  15.7 us (1%)
    all_gather x2, waiting for transfers between devices, gather_rows(): return lax.all_gather(values, 'tensor', axis=0, tiled=True)  166 us
    reduce_scatter x2, waiting for transfers between devices, input_total(): lax.psum_scatter(term_fn(jnp.int32(0), short_rows * lax.axis_size('tensor...  154 us
    all_gather x2, waiting for transfers between devices, gather_cotangent(): return lax.all_gather(values, 'tensor', axis=0, tiled=True)  116 us
    reduce_scatter x2, waiting for transfers between devices, branch_total(): lax.psum_scatter(term_fn(jnp.int32(0), short_rows * lax.axis_size('tensor...  108 us
    reduce_scatter x1, waiting for transfers between devices, body(): lax.psum_scatter(gate_grad.astype(jnp.bfloat16), 'dp', scatter_dimension=...  62.6 us
    dot_general x7, matrix products, weight_term(): jnp.einsum('lsd,lsc->dc', rows_in, grads_in, preferred_element_type=jnp.f...  49.8 us
    psum x1, blocking collectives, body(): lax.psum((jnp.sum(gain_one_terms, axis=(0, 1)), jnp.sum(gain_two_terms, a...  46.5 us
    all_gather x1, waiting for transfers between devices, fetch_feedforward(): lax.all_gather(down_weight, 'dp', axis=0, tiled=True)  45.8 us
  transfers between devices with their start and end apart: 22, of which 20 were waited for; matrix products, arithmetic and copies ran while one was open for 16% of the time, Pallas kernels for 0%

commit v1 on v0

--- a/solution.py
+++ b/solution.py
@@ -5,6 +5,24 @@
 
 epsilon = 1e-06
 rope_base = 1000000.0
+
+
+def gather_around(value, axis, dim):
+    ways, here, turn = (lax.axis_size(axis), lax.axis_index(axis), value.shape[dim])
+    shape = [n * ways if d == dim else n for d, n in enumerate(value.shape)]
+    full = lax.dynamic_update_slice_in_dim(
+        jnp.zeros(shape, value.dtype), value, here * turn, axis=dim
+    )
+    going_up = going_down = value
+    for far in range(1, ways // 2 + 1):
+        going_up = lax.ppermute(going_up, axis, [(d, (d + 1) % ways) for d in range(ways)])
+        full = lax.dynamic_update_slice_in_dim(full, going_up, (here - far) % ways * turn, axis=dim)
+        if 2 * far < ways:
+            going_down = lax.ppermute(going_down, axis, [(d, (d - 1) % ways) for d in range(ways)])
+            full = lax.dynamic_update_slice_in_dim(
+                full, going_down, (here + far) % ways * turn, axis=dim
+            )
+    return full
 
 
 def rms_parts(values, gain):
@@ -123,7 +141,7 @@
 
 
 def gather_cotangent(values):
-    return lax.all_gather(values, "tensor", axis=0, tiled=True)
+    return gather_around(values, "tensor", 0)
 
 
 def branch_total(term_fn, short_rows):

time: 1340 us -> 1190 us (0.89)
  waiting for transfers between devices: 986 us -> 781 us
  starting transfers between devices: 1.52 us -> 49.7 us
    all_gather x2 -> x0, waiting for transfers between devices: 116 us -> none  [gather_cotangent(): return lax.all_gather(values, 'tensor', axis=0, tiled=True)]
    ppermute x0 -> x6, waiting for transfers between devices: none -> 104 us  [the longest x4 102 us: gather_around(): lax.ppermute(going_up, axis, [(d, (d + 1) % ways) for d in range(ways)])]
    reduce_scatter x1, waiting for transfers between devices: 62.6 us -> 0.02 us  [body(): lax.psum_scatter(gate_grad.astype(jnp.bfloat16), 'dp', scatter_dimension=...]
    ppermute x0 -> x6, starting transfers between devices: none -> 48.1 us  [the longest x4 43.4 us: gather_around(): lax.ppermute(going_up, axis, [(d, (d + 1) % ways) for d in range(ways)])]
    all_gather x1, waiting for transfers between devices: 41.5 us -> 0.01 us  [fetch_feedforward(): lax.all_gather(up_weight, 'dp', axis=0, tiled=True)]
    reduce_scatter x2, waiting for transfers between devices: 154 us -> 119 us  [input_total(): lax.psum_scatter(term_fn(jnp.int32(0), short_rows * lax.axis_size('tensor...]
    all_gather x2, waiting for transfers between devices: 166 us -> 133 us  [gather_rows(): return lax.all_gather(values, 'tensor', axis=0, tiled=True)]
    reduce_scatter x1, waiting for transfers between devices: 30.6 us -> 0.01 us  [body(): lax.psum_scatter(up_grad.astype(jnp.bfloat16), 'dp', scatter_dimension=0,...]
  transfers between devices with their start and end apart: 22 -> 26, of which waited for: 20 -> 21; matrix products, arithmetic and copies ran while one was open for 16% -> 19% of each run, Pallas kernels for 0% -> 0%
where the time goes in v1:
time: 1190 us; the launch traced here: 1180 us
  waiting for transfers between devices  781 us (66%)
  matrix products  191 us (16%)
  other arithmetic  65.7 us (6%)
  starting transfers between devices  49.7 us (4%)
  blocking collectives  46.4 us (4%)
  local copies, waits for them, and re-layouts  30.8 us (3%)
  between operations  15.6 us (1%)
    all_gather x2, waiting for transfers between devices, gather_rows(): return lax.all_gather(values, 'tensor', axis=0, tiled=True)  133 us
    reduce_scatter x2, waiting for transfers between devices, input_total(): lax.psum_scatter(term_fn(jnp.int32(0), short_rows * lax.axis_size('tensor...  119 us
    reduce_scatter x2, waiting for transfers between devices, branch_total(): lax.psum_scatter(term_fn(jnp.int32(0), short_rows * lax.axis_size('tensor...  108 us
    ppermute x4, waiting for transfers between devices, gather_around(): lax.ppermute(going_up, axis, [(d, (d + 1) % ways) for d in range(ways)])  102 us
    dot_general x7, matrix products, weight_term(): jnp.einsum('lsd,lsc->dc', rows_in, grads_in, preferred_element_type=jnp.f...  49.2 us
    psum x1, blocking collectives, body(): lax.psum((jnp.sum(gain_one_terms, axis=(0, 1)), jnp.sum(gain_two_terms, a...  46.4 us
    dot_general x7, matrix products, project_rows(): jnp.einsum('lsc,dc->lsd', left, right, preferred_element_type=jnp.float32)  44.6 us
    ppermute x4, starting transfers between devices, gather_around(): lax.ppermute(going_up, axis, [(d, (d + 1) % ways) for d in range(ways)])  43.4 us
  transfers between devices with their start and end apart: 26, of which 21 were waited for; matrix products, arithmetic and copies ran while one was open for 19% of the time, Pallas kernels for 0%

profile of v1, /device:TPU:0, one launch (start us, length us, event | category | flops | bytes accessed | tf_op | source)
XLA Modules:
  0.0 1179.6 jit_solution(1215502734976418746)
XLA Ops:
  14.9 2.7 fusion.90
  19.1 16.9 %all-gather.12.cloned.1.call-done = bf16[2048,256]{1,0:T(8,128)(2,1)} async-done(((bf16[256,256]{1,0:T(8,128)(2,1)}), bf16[2048,256]{1,0:T(8,128)(2,1)}) %all-gather.12.cloned.1.call-update) | async-done | bytes 1048592 | tf_op jit(solution)/shard_map/all_gather | solution.py:126
  38.3 23.0 %all-gather.14.cloned.1.call-done = bf16[2048,256]{1,0:T(8,128)(2,1)} async-done(((bf16[256,256]{1,0:T(8,128)(2,1)}), bf16[2048,256]{1,0:T(8,128)(2,1)}) %all-gather.14.cloned.1.call-update) | async-done | bytes 1048592 | tf_op jit(solution)/shard_map/all_gather | solution.py:125
  61.3 82.9 %all-gather.10.cloned.1.call-done = bf16[1024,1,2048]{2,0,1:T(8,128)(2,1)} async-done(((bf16[256,1,2048]{2,0,1:T(8,128)(2,1)}), bf16[1024,1,2048]{2,0,1:T(8,128)(2,1)}) %all-gather.10.cloned.1.call-update) | async-done | bytes 4194320 | tf_op jit(solution)/shard_map/all_gather | solution.py:140
  144.2 3.8 fusion.25
  149.5 22.8 %all-gather.16.cloned.1.call-done = bf16[2048,512]{1,0:T(8,128)(2,1)} async-done(((bf16[256,512]{1,0:T(8,128)(2,1)}), bf16[2048,512]{1,0:T(8,128)(2,1)}) %all-gather.16.cloned.1.call-update) | async-done | bytes 2097168 | tf_op jit(solution)/shard_map/all_gather | solution.py:124
  172.3 5.2 fusion.23
  184.5 7.8 fusion.94
  192.2 8.0 fusion.3
  200.3 7.6 fusion.66
  208.9 6.0 convert_bitcast_fusion.1
  215.8 76.4 %reduce-scatter.12.cloned.1.call-done = bf16[256,1,2048]{2,0,1:T(8,128)(2,1)} async-done(((bf16[1024,1,2048]{2,0,1:T(8,128)(2,1)}), bf16[256,1,2048]{2,0,1:T(8,128)(2,1)}) %reduce-scatter.12.cloned.1.call-update) | async-done | bytes 1048592 | tf_op jit(solution)/shard_map/reduce_scatter | solution.py:148
  301.7 24.1 %collective-permute-done = bf16[256,1,2048]{2,0,1:T(8,128)(2,1)S(1)} collective-permute-done((bf16[256,1,2048]{2,0,1:T(8,128)(2,1)S(1)}, bf16[256,1,2048]{2,0,1:T(8,128)(2,1)S(1)}, u32[]{:S(2)}, u32[]{:S(2)}) %collective-permute-start) | collective-permute-done | bytes 1048608 | tf_op jit(solution)/shard_map/ppermute | solution.py:18
  325.8 20.1 %collective-permute-start.2 = (bf16[256,1,2048]{2,0,1:T(8,128)(2,1)S(1)}, bf16[256,1,2048]{2,0,1:T(8,128)(2,1)}, u32[]{:S(2)}, u32[]{:S(2)}) collective-permute-start(bf16[256,1,2048]{2,0,1:T(8,128)(2,1)S(1)} %collective-permute-done), channel_id=1, source_target_pairs={{0,1},{1,2},{2,3},{3,0},{4,5},{5,6},{6,7},{7,4},{8,9},{9,10},{10,1... | collective-permute-start | bytes 3145736 | tf_op jit(solution)/shard_map/ppermute | solution.py:18
  352.8 32.4 %collective-permute-done.2 = bf16[256,1,2048]{2,0,1:T(8,128)(2,1)} collective-permute-done((bf16[256,1,2048]{2,0,1:T(8,128)(2,1)S(1)}, bf16[256,1,2048]{2,0,1:T(8,128)(2,1)}, u32[]{:S(2)}, u32[]{:S(2)}) %collective-permute-start.2) | collective-permute-done | bytes 1048608 | tf_op jit(solution)/shard_map/ppermute | solution.py:18
  387.5 49.9 %all-gather.20.cloned.1.call-done = bf16[1024,1,2048]{2,0,1:T(8,128)(2,1)} async-done(((bf16[256,1,2048]{2,0,1:T(8,128)(2,1)}), bf16[1024,1,2048]{2,0,1:T(8,128)(2,1)}) %all-gather.20.cloned.1.call-update) | async-done | bytes 4194320 | tf_op jit(solution)/shard_map/all_gather | solution.py:140
  437.4 11.9 %fusion.13 = f32[1024,1536]{1,0:T(8,128)} fusion(bf16[2048,1536]{1,0:T(8,128)(2,1)} %all-gather.24.cloned.1.call-done, bf16[1024,1,2048]{2,0,1:T(8,128)(2,1)} %all-gather.20.cloned.1.call-done), kind=kOutput, calls=%fused_computation.27 | convolution fusion | flops 6442450944 | bytes 16777216 | tf_op jit(solution)/shard_map/qpt,to->qpo/dot_general | solution.py:248
  449.3 35.0 %all-gather.22.cloned.1.call-done = bf16[2048,1536]{1,0:T(8,128)(2,1)} async-done(((bf16[256,1536]{1,0:T(8,128)(2,1)}), bf16[2048,1536]{1,0:T(8,128)(2,1)}) %all-gather.22.cloned.1.call-update) | async-done | bytes 6291472 | tf_op jit(solution)/shard_map/all_gather | solution.py:133
  484.3 11.7 fusion.15
  496.0 35.4 %all-gather.26.cloned.1.call-done = bf16[2048,1536]{1,0:T(8,128)(2,1)} async-done(((bf16[256,1536]{1,0:T(8,128)(2,1)}), bf16[2048,1536]{1,0:T(8,128)(2,1)}) %all-gather.26.cloned.1.call-update) | async-done | bytes 6291472 | tf_op jit(solution)/shard_map/all_gather | solution.py:135
  531.5 17.3 %multiply_convert_fusion = (bf16[1024,1536]{1,0:T(8,128)(2,1)}, bf16[1024,1536]{1,0:T(8,128)(2,1)}, bf16[1024,1536]{1,0:T(8,128)(2,1)}) fusion(f32[1024,1536]{1,0:T(8,128)} %fusion.15, f32[1024,1536]{1,0:T(8,128)} %fusion.13, bf16[1024,2048]{1,0:T(8,128)(2,1)} %bitcast_dynamic-update-slice_fusion.4, bf16[2048,1536]{1,0:T(8,128)(2,1)} %all-gather.26.cloned.1.call-done), kind=kOutput, calls=%fused_computation.19 | convolution fusion | flops 6466043904 | bytes 32505856 | tf_op jit(solution)/shard_map/qpt,to->qpo/dot_general | solution.py:262
  548.8 8.7 fusion.95
  557.6 11.2 fusion.10
  568.8 11.5 convolution_convert_fusion.2
  580.4 11.7 convolution_convert_fusion.1
  592.1 11.5 convolution_convert_fusion
  603.7 42.0 %reduce-scatter.16.cloned.1.call-done = bf16[256,1,2048]{2,0,1:T(8,128)(2,1)} async-done(((bf16[1024,1,2048]{2,0,1:T(8,128)(2,1)}), bf16[256,1,2048]{2,0,1:T(8,128)(2,1)}) %reduce-scatter.16.cloned.1.call-update) | async-done | bytes 1048592 | tf_op jit(solution)/shard_map/reduce_scatter | solution.py:157
  653.5 24.1 %collective-permute-done.3 = bf16[256,1,2048]{2,0,1:T(8,128)(2,1)S(1)} collective-permute-done((bf16[256,1,2048]{2,0,1:T(8,128)(2,1)S(1)}, bf16[256,1,2048]{2,0,1:T(8,128)(2,1)S(1)}, u32[]{:S(2)}, u32[]{:S(2)}) %collective-permute-start.3) | collective-permute-done | bytes 1048608 | tf_op jit(solution)/shard_map/ppermute | solution.py:18
  677.6 20.3 %collective-permute-start.5 = (bf16[256,1,2048]{2,0,1:T(8,128)(2,1)S(1)}, bf16[256,1,2048]{2,0,1:T(8,128)(2,1)S(1)}, u32[]{:S(2)}, u32[]{:S(2)}) collective-permute-start(bf16[256,1,2048]{2,0,1:T(8,128)(2,1)S(1)} %collective-permute-done.3), channel_id=1, source_target_pairs={{0,1},{1,2},{2,3},{3,0},{4,5},{5,6},{6,7},{7,4},{8,9},{9,10},{10,1... | collective-permute-start | bytes 3145736 | tf_op jit(solution)/shard_map/ppermute | solution.py:18
  699.9 21.2 %collective-permute-done.5 = bf16[256,1,2048]{2,0,1:T(8,128)(2,1)S(1)} collective-permute-done((bf16[256,1,2048]{2,0,1:T(8,128)(2,1)S(1)}, bf16[256,1,2048]{2,0,1:T(8,128)(2,1)S(1)}, u32[]{:S(2)}, u32[]{:S(2)}) %collective-permute-start.5) | collective-permute-done | bytes 1048608 | tf_op jit(solution)/shard_map/ppermute | solution.py:18
  727.5 7.5 fusion
  735.0 11.0 fusion.2
  746.0 6.4 fusion.74
  759.1 9.2 fusion.75
  771.7 6.0 convolution_convert_fusion.3
  778.0 4.7 fusion.67
  793.2 3.7 fusion.35
  801.4 3.8 fusion.30
  805.4 11.2 convert_bitcast_fusion
  821.8 19.6 %reduce-scatter.32.cloned.1.call-done = bf16[256,1536]{1,0:T(8,128)(2,1)} async-done(((bf16[2048,1536]{1,0:T(8,128)(2,1)}), bf16[256,1536]{1,0:T(8,128)(2,1)}) %reduce-scatter.32.cloned.1.call-update) | async-done | bytes 786448 | tf_op jit(solution)/shard_map/reduce_scatter | solution.py:355
  843.9 36.6 %reduce-scatter.22.cloned.1.call-done = bf16[256,256]{1,0:T(8,128)(2,1)} async-done(((bf16[2048,256]{1,0:T(8,128)(2,1)}), bf16[256,256]{1,0:T(8,128)(2,1)}) %reduce-scatter.22.cloned.1.call-update) | async-done | bytes 131088 | tf_op jit(solution)/shard_map/reduce_scatter | solution.py:340
  882.1 37.4 %reduce-scatter.24.cloned.1.call-done = bf16[256,256]{1,0:T(8,128)(2,1)} async-done(((bf16[2048,256]{1,0:T(8,128)(2,1)}), bf16[256,256]{1,0:T(8,128)(2,1)}) %reduce-scatter.24.cloned.1.call-update) | async-done | bytes 131088 | tf_op jit(solution)/shard_map/reduce_scatter | solution.py:343
  921.1 42.6 %reduce-scatter.26.cloned.1.call-done = bf16[256,512]{1,0:T(8,128)(2,1)} async-done(((bf16[2048,512]{1,0:T(8,128)(2,1)}), bf16[256,512]{1,0:T(8,128)(2,1)}) %reduce-scatter.26.cloned.1.call-update) | async-done | bytes 262160 | tf_op jit(solution)/shard_map/reduce_scatter | solution.py:346
  965.5 42.5 %reduce-scatter.20.cloned.1.call-done = bf16[256,512]{1,0:T(8,128)(2,1)} async-done(((bf16[2048,512]{1,0:T(8,128)(2,1)}), bf16[256,512]{1,0:T(8,128)(2,1)}) %reduce-scatter.20.cloned.1.call-update) | async-done | bytes 262160 | tf_op jit(solution)/shard_map/reduce_scatter | solution.py:337
  1009.8 77.3 %reduce-scatter.18.cloned.1.call-done = bf16[256,1,2048]{2,0,1:T(8,128)(2,1)} async-done(((bf16[1024,1,2048]{2,0,1:T(8,128)(2,1)}), bf16[256,1,2048]{2,0,1:T(8,128)(2,1)}) %reduce-scatter.18.cloned.1.call-update) | async-done | bytes 1048592 | tf_op jit(solution)/shard_map/reduce_scatter | solution.py:157
  1089.2 46.4 %all-reduce = (f32[2048]{0:T(1024)}, f32[128]{0:T(128)}, f32[128]{0:T(128)}, f32[2048]{0:T(1024)}) all-reduce(f32[2048]{0:T(1024)S(1)} %get-tuple-element.17, f32[128]{0:T(128)S(1)} %get-tuple-element.13, f32[128]{0:T(128)S(1)} %get-tuple-element.19, f32[2048]{0:T(1024)S(1)} %get-tuple-element.15), channel_id=1, replica_groups=mesh['dp'=8,'tensor'=4] {'dp','tensor'}, use_global_device_ids=true, to_apply=%region_16.17 | all-reduce | flops 4352 | bytes 34816 | tf_op jit(solution)/shard_map/psum | solution.py:327
  1135.5 32.1 %reduce-scatter.14.cloned.1.call-done = bf16[256,1,2048]{2,0,1:T(8,128)(2,1)} async-done(((bf16[1024,1,2048]{2,0,1:T(8,128)(2,1)}), bf16[256,1,2048]{2,0,1:T(8,128)(2,1)}) %reduce-scatter.14.cloned.1.call-update) | async-done | bytes 1048592 | tf_op jit(solution)/shard_map/reduce_scatter | solution.py:148
  1167.6 4.8 fusion.49
  (261 shorter events, 97.8 us)
Async XLA Ops:
  7.2 7.6 copy-start.63
  7.2 10.4 copy-start.64
  7.2 10.4 copy-start.48
  7.2 28.8 %all-gather.12.cloned.1.call-start = ((), (), s32[]{:S(2)}) async-start(), calls=%async_computation.12 | async-start | bytes 1179648 | tf_op jit(solution)/shard_map/all_gather | solution.py:126
  7.9 53.4 %all-gather.14.cloned.1.call-start = ((), (), s32[]{:S(2)}) async-start(), calls=%async_computation.13 | async-start | bytes 1179648 | tf_op jit(solution)/shard_map/all_gather | solution.py:125
  8.7 135.5 %all-gather.10.cloned.1.call-start = ((), (), s32[]{:S(2)}) async-start(), calls=%async_computation.11 | async-start | bytes 5242880 | tf_op jit(solution)/shard_map/all_gather | solution.py:140
  13.5 158.8 %all-gather.16.cloned.1.call-start = ((), (), s32[]{:S(2)}) async-start(), calls=%async_computation.14 | async-start | bytes 2359296 | tf_op jit(solution)/shard_map/all_gather | solution.py:124
  14.1 193.9 %all-gather.18.cloned.1.call-start = ((), (), s32[]{:S(2)}) async-start(), calls=%async_computation.15 | async-start | bytes 2359296 | tf_op jit(solution)/shard_map/all_gather | solution.py:127
  14.7 277.5 %reduce-scatter.12.cloned.1.call-start = ((), (), s32[]{:S(2)}) async-start(), calls=%async_computation.16 | async-start | bytes 5242880 | tf_op jit(solution)/shard_map/reduce_scatter | solution.py:148
  14.8 164.0 %copy-start.53 = (f32[128]{0:T(128)}, f32[128]{0:T(128)S(1)}, u32[]{:S(2)}) copy-start(f32[128]{0:T(128)S(1)} %convert_element_type.240) | copy-start | bytes 1540
  17.5 162.7 %copy-start.51 = (f32[128]{0:T(128)}, f32[128]{0:T(128)S(1)}, u32[]{:S(2)}) copy-start(f32[128]{0:T(128)S(1)} %convert_element_type.242) | copy-start | bytes 1540
  148.0 30.7 %copy-start.3 = (f32[1024,256]{0,1:T(8,128)}, f32[1024,256]{0,1:T(8,128)S(1)}, u32[]{:S(2)}) copy-start(f32[1024,256]{0,1:T(8,128)S(1)} %fusion.25) | copy-start | bytes 3145732
  148.2 30.6 %copy-start.42 = (f32[1024,2]{0,1:T(2,128)}, f32[1024,2]{0,1:T(2,128)S(1)}, u32[]{:S(2)}) copy-start(f32[1024,2]{0,1:T(2,128)S(1)} %add_rsqrt_fusion.1) | copy-start | bytes 24580
  184.4 15.8 %copy-start.38 = (bf16[1024,2,128,1]{2,0,3,1:T(8,128)(2,1)}, bf16[1024,2,128,1]{2,0,3,1:T(8,128)(2,1)S(1)}, u32[]{:S(2)}) copy-start(bf16[1024,2,128,1]{2,0,3,1:T(8,128)(2,1)S(1)} %fusion.81) | copy-start | bytes 1572868
  214.9 77.2 %copy-start.2 = (bf16[256,1,2048]{2,0,1:T(8,128)(2,1)S(1)}, bf16[256,1,2048]{2,0,1:T(8,128)(2,1)}, u32[]{:S(2)}) copy-start(bf16[256,1,2048]{2,0,1:T(8,128)(2,1)} %param.14) | copy-start | bytes 3145732
  215.0 82.8 %copy-start.18 = (bf16[256,1,2048]{2,0,1:T(8,128)(2,1)S(1)}, bf16[256,1,2048]{2,0,1:T(8,128)(2,1)}, u32[]{:S(2)}) copy-start(bf16[256,1,2048]{2,0,1:T(8,128)(2,1)} %param.27) | copy-start | bytes 3145732
  215.0 172.5 %all-gather.24.cloned.1.call-start = ((), (), s32[]{:S(2)}) async-start(), calls=%async_computation.19 | async-start | bytes 7077888 | tf_op jit(solution)/shard_map/all_gather | solution.py:134
  215.7 221.7 %all-gather.20.cloned.1.call-start = ((), (), s32[]{:S(2)}) async-start(), calls=%async_computation.17 | async-start | bytes 5242880 | tf_op jit(solution)/shard_map/all_gather | solution.py:140
  296.4 187.9 %all-gather.22.cloned.1.call-start = ((), (), s32[]{:S(2)}) async-start(), calls=%async_computation.18 | async-start | bytes 7077888 | tf_op jit(solution)/shard_map/all_gather | solution.py:133
  297.2 234.3 %all-gather.26.cloned.1.call-start = ((), (), s32[]{:S(2)}) async-start(), calls=%async_computation.20 | async-start | bytes 7077888 | tf_op jit(solution)/shard_map/all_gather | solution.py:135
  297.8 348.0 %reduce-scatter.16.cloned.1.call-start = ((), (), s32[]{:S(2)}) async-start(), calls=%async_computation.22 | async-start | bytes 5242880 | tf_op jit(solution)/shard_map/reduce_scatter | solution.py:157
  297.8 28.0 %collective-permute-start = (bf16[256,1,2048]{2,0,1:T(8,128)(2,1)S(1)}, bf16[256,1,2048]{2,0,1:T(8,128)(2,1)S(1)}, u32[]{:S(2)}, u32[]{:S(2)}) collective-permute-start(bf16[256,1,2048]{2,0,1:T(8,128)(2,1)S(1)} %copy-done.18), channel_id=1, source_target_pairs={{0,1},{1,2},{2,3},{3,0},{4,5},{5,6},{6,7},{7,4},{8,9},{9,10},{10,1... | collective-permute-start | bytes 3145736 | tf_op jit(solution)/shard_map/ppermute | solution.py:18
  299.4 51.1 %collective-permute-start.1 = (bf16[256,1,2048]{2,0,1:T(8,128)(2,1)S(1)}, bf16[256,1,2048]{2,0,1:T(8,128)(2,1)}, u32[]{:S(2)}, u32[]{:S(2)}) collective-permute-start(bf16[256,1,2048]{2,0,1:T(8,128)(2,1)S(1)} %copy-done.18), channel_id=1, source_target_pairs={{0,3},{1,0},{2,1},{3,2},{4,7},{5,4},{6,5},{7,6},{8,11},{9,8},{10,9... | collective-permute-start | bytes 3145736 | tf_op jit(solution)/shard_map/ppermute | solution.py:21
  325.8 59.4 %collective-permute-start.2 = (bf16[256,1,2048]{2,0,1:T(8,128)(2,1)S(1)}, bf16[256,1,2048]{2,0,1:T(8,128)(2,1)}, u32[]{:S(2)}, u32[]{:S(2)}) collective-permute-start(bf16[256,1,2048]{2,0,1:T(8,128)(2,1)S(1)} %collective-permute-done), channel_id=1, source_target_pairs={{0,1},{1,2},{2,3},{3,0},{4,5},{5,6},{6,7},{7,4},{8,9},{9,10},{10,1... | collective-permute-start | bytes 3145736 | tf_op jit(solution)/shard_map/ppermute | solution.py:18
  531.5 17.3 %copy-start.56 = (bf16[2048,1536]{1,0:T(8,128)(2,1)S(1)}, bf16[2048,1536]{1,0:T(8,128)(2,1)}, u32[]{:S(2)}) copy-start(bf16[2048,1536]{1,0:T(8,128)(2,1)} %all-gather.22.cloned.1.call-done) | copy-start | bytes 18874372
  548.8 8.7 copy-start.67
  568.8 247.9 %reduce-scatter.28.cloned.1.call-start = ((), (), s32[]{:S(2)}) async-start(), calls=%async_computation.28 | async-start | bytes 7077888 | tf_op jit(solution)/shard_map/reduce_scatter | solution.py:349
  580.3 238.8 %reduce-scatter.30.cloned.1.call-start = ((), (), s32[]{:S(2)}) async-start(), calls=%async_computation.29 | async-start | bytes 7077888 | tf_op jit(solution)/shard_map/reduce_scatter | solution.py:352
  592.1 249.3 %reduce-scatter.32.cloned.1.call-start = ((), (), s32[]{:S(2)}) async-start(), calls=%async_computation.30 | async-start | bytes 7077888 | tf_op jit(solution)/shard_map/reduce_scatter | solution.py:355
  603.6 42.1 %copy-start.7 = (bf16[256,1,2048]{2,0,1:T(8,128)(2,1)S(1)}, bf16[256,1,2048]{2,0,1:T(8,128)(2,1)}, u32[]{:S(2)}) copy-start(bf16[256,1,2048]{2,0,1:T(8,128)(2,1)} %reduce-scatter.12.cloned.1.call-done) | copy-start | bytes 3145732
  603.7 276.8 %reduce-scatter.22.cloned.1.call-start = ((), (), s32[]{:S(2)}) async-start(), calls=%async_computation.25 | async-start | bytes 1179648 | tf_op jit(solution)/shard_map/reduce_scatter | solution.py:340
  648.5 75.2 %slice-start = ((s8[16777216]{0:T(1024)(128)(4,1)}), s8[4194304]{0:T(1024)(128)(4,1)S(1)}, s32[]{:S(2)}) async-start(s8[16777216]{0:T(1024)(128)(4,1)} %bitcast.221), calls=%async_computation.31 | async-start | bytes 8388608
  649.6 71.6 %copy-start.62 = (bf16[2048,512]{1,0:T(8,128)(2,1)S(1)}, bf16[2048,512]{1,0:T(8,128)(2,1)}, u32[]{:S(2)}) copy-start(bf16[2048,512]{1,0:T(8,128)(2,1)} %all-gather.18.cloned.1.call-done) | copy-start | bytes 6291460
  649.7 28.0 %collective-permute-start.3 = (bf16[256,1,2048]{2,0,1:T(8,128)(2,1)S(1)}, bf16[256,1,2048]{2,0,1:T(8,128)(2,1)S(1)}, u32[]{:S(2)}, u32[]{:S(2)}) collective-permute-start(bf16[256,1,2048]{2,0,1:T(8,128)(2,1)S(1)} %get-tuple-element.27), channel_id=1, source_target_pairs={{0,1},{1,2},{2,3},{3,0},{4,5},{5,6},{6,7},{7,4},{8,9},{9,10},{10,1... | collective-permute-start | bytes 3145736 | tf_op jit(solution)/shard_map/ppermute | solution.py:18
  651.2 48.6 %collective-permute-start.4 = (bf16[256,1,2048]{2,0,1:T(8,128)(2,1)S(1)}, bf16[256,1,2048]{2,0,1:T(8,128)(2,1)S(1)}, u32[]{:S(2)}, u32[]{:S(2)}) collective-permute-start(bf16[256,1,2048]{2,0,1:T(8,128)(2,1)S(1)} %get-tuple-element.27), channel_id=1, source_target_pairs={{0,3},{1,0},{2,1},{3,2},{4,7},{5,4},{6,5},{7,6},{8,11},{9,8},{10,9... | collective-permute-start | bytes 3145736 | tf_op jit(solution)/shard_map/ppermute | solution.py:21
  677.6 43.5 %collective-permute-start.5 = (bf16[256,1,2048]{2,0,1:T(8,128)(2,1)S(1)}, bf16[256,1,2048]{2,0,1:T(8,128)(2,1)S(1)}, u32[]{:S(2)}, u32[]{:S(2)}) collective-permute-start(bf16[256,1,2048]{2,0,1:T(8,128)(2,1)S(1)} %collective-permute-done.3), channel_id=1, source_target_pairs={{0,1},{1,2},{2,3},{3,0},{4,5},{5,6},{6,7},{7,4},{8,9},{9,10},{10,1... | collective-permute-start | bytes 3145736 | tf_op jit(solution)/shard_map/ppermute | solution.py:18
  698.0 25.7 %slice-start.1 = ((s8[16777216]{0:T(1024)(128)(4,1)}), s8[4194304]{0:T(1024)(128)(4,1)S(1)}, s32[]{:S(2)}) async-start(s8[16777216]{0:T(1024)(128)(4,1)} %bitcast.221), calls=%async_computation.32 | async-start | bytes 8388608
  735.0 11.0 copy-start.22
  758.7 160.8 %reduce-scatter.24.cloned.1.call-start = ((), (), s32[]{:S(2)}) async-start(), calls=%async_computation.26 | async-start | bytes 1179648 | tf_op jit(solution)/shard_map/reduce_scatter | solution.py:343
  759.1 10.1 copy-start.59
  771.6 192.1 %reduce-scatter.26.cloned.1.call-start = ((), (), s32[]{:S(2)}) async-start(), calls=%async_computation.27 | async-start | bytes 2359296 | tf_op jit(solution)/shard_map/reduce_scatter | solution.py:346
  777.7 230.3 %reduce-scatter.20.cloned.1.call-start = ((), (), s32[]{:S(2)}) async-start(), calls=%async_computation.24 | async-start | bytes 2359296 | tf_op jit(solution)/shard_map/reduce_scatter | solution.py:337
  796.9 290.2 %reduce-scatter.18.cloned.1.call-start = ((), (), s32[]{:S(2)}) async-start(), calls=%async_computation.23 | async-start | bytes 5242880 | tf_op jit(solution)/shard_map/reduce_scatter | solution.py:157
  805.2 362.5 %reduce-scatter.14.cloned.1.call-start = ((), (), s32[]{:S(2)}) async-start(), calls=%async_computation.21 | async-start | bytes 5242880 | tf_op jit(solution)/shard_map/reduce_scatter | solution.py:148
  816.6 270.5 %copy-start.47 = (f32[2048]{0:T(1024)S(1)}, f32[2048]{0:T(1024)}, u32[]{:S(2)}) copy-start(f32[2048]{0:T(1024)} %copy-done.46) | copy-start | bytes 24580
  816.6 270.5 %copy-start.50 = (f32[256]{0:T(256)S(1)}, f32[256]{0:T(256)}, u32[]{:S(2)}) copy-start(f32[256]{0:T(256)} %copy-done.49) | copy-start | bytes 3076
  819.1 348.5 %copy-start.8 = (bf16[256,1,2048]{2,0,1:T(8,128)(2,1)S(1)}, bf16[256,1,2048]{2,0,1:T(8,128)(2,1)}, u32[]{:S(2)}) copy-start(bf16[256,1,2048]{2,0,1:T(8,128)(2,1)} %reduce-scatter.12.cloned.1.call-done) | copy-start | bytes 3145732
  819.1 348.5 %copy-start.19 = (bf16[256,1,2048]{2,0,1:T(8,128)(2,1)S(1)}, bf16[256,1,2048]{2,0,1:T(8,128)(2,1)}, u32[]{:S(2)}) copy-start(bf16[256,1,2048]{2,0,1:T(8,128)(2,1)} %param.27) | copy-start | bytes 3145732
  (50 other events, 141.5 us)
Sparse Core Ops, SparseCore 0:
  9.9 26.0 all-gather.11
  37.9 23.3 all-gather.13
  63.5 80.7 all-gather.9
  146.0 26.2 all-gather.15
  174.0 27.7 all-gather.17
  215.1 77.0 reduce-scatter.11
  294.1 45.9 all-gather.23
  342.1 95.2 all-gather.19
  439.3 44.9 all-gather.21
  486.0 45.3 all-gather.25
  568.9 76.7 reduce-scatter.15
  649.0 62.2 reduce-scatter.27
  714.6 61.7 reduce-scatter.29
  779.6 61.7 reduce-scatter.31
  844.4 35.9 reduce-scatter.21
  883.5 35.9 reduce-scatter.23
  922.6 41.0 reduce-scatter.25
  966.9 41.0 reduce-scatter.19
  1010.3 76.7 reduce-scatter.17
  1089.3 78.3 reduce-scatter.13
